TPU v7x, 256 devices: a whole 4x4x8 slice. The times are simulated.
256 devices in a mesh: group: 8 (over z_hi, y), shard: 32 (over x, z_lo, core).
Axes of the slice: x: 4, y: 4, z: 8 (z_hi: 2, z_lo: 4; z = z_hi * 4 + z_lo), core: 2. Of those that a mesh axis runs over, the one named last changes fastest.
Arguments:
- gradients: bfloat16 [8, 32, 256, 8192], P('group', 'shard'), may hold values from -1.59375 to 1.59375
- momentum: float32 [8, 256, 8192], P('group', None, 'shard'), may hold values from -6 to 6
- master: float32 [256, 8192], P(None, 'shard'), may hold values from -0.6 to 0.6
- indices: int32 [8, 4, 128, 32], P('group', None, 'shard'), may hold values from 0 to 4095, as said below
Outputs:
- momentum_out: float32 [8, 256, 8192], P('group', None, 'shard')
- master_out: float32 [256, 8192], P(None, 'shard')
- params_full: bfloat16 [256, 8192], replicated
Inputs may be any that keep to these rules, and one draw needn't show every extreme that they name: `indices`: the 32 positions of one group and block are distinct.
All inputs are finite; a program needn't handle non-finite values.
Results may differ from a plain program's by a relative error of at most 0.001.
Values may be sent and summed in bfloat16 or wider, within the bound.
No kernel may reach another device: no remote copies, remote signals or barrier semaphores. Data moves between devices by JAX's collectives and lax.ppermute only.
A program may use at most 128 MiB of HBM per device.

v0:
```python
import jax
import jax.numpy as jnp
from jax import lax
from jax.sharding import Mesh
from jax.sharding import PartitionSpec as P

BLOCK = 64
SHARD = ("shard_0", "shard_1", "shard_2")
momentum_decay = 0.9
step_rate = 0.5


def in_blocks(shard, dim, peers):
    before, after = (shard.shape[:dim], shard.shape[dim + 1 :])
    return jnp.moveaxis(shard.reshape(*before, peers, -1, *after), dim, 0)


def summed_rows(shard, chips, core, dim):
    sizes = (lax.axis_size(chips), lax.axis_size(core))
    parts = in_blocks(shard, dim, sizes[0] * sizes[1])
    inside = parts.shape[1:]
    parts = parts.reshape(*sizes, *inside).swapaxes(0, 1).reshape(-1, *inside)
    parts = lax.psum_scatter(parts, core, scatter_dimension=0, tiled=True)
    return lax.psum_scatter(parts, chips, scatter_dimension=0, tiled=True)[0]


def joined_along(parts, dim):
    parts = jnp.moveaxis(parts, 0, dim)
    shape = parts.shape
    return parts.reshape(*shape[:dim], shape[dim] * shape[dim + 1], *shape[dim + 2 :])


def copy_for_each(shard, axis):
    peers = lax.axis_size(axis)
    return lax.all_to_all(
        jnp.broadcast_to(shard[None], (peers, *shard.shape)), axis, 0, 0, tiled=True
    )


def gathered_copies(shard, axis, dim):
    return joined_along(copy_for_each(shard, axis), dim)


def cosine_table(side):
    freqs = jnp.arange(side, dtype=jnp.float32)[:, None]
    places = jnp.arange(side, dtype=jnp.float32)[None, :]
    table = jnp.cos(jnp.pi * (2.0 * places + 1.0) * freqs / (2.0 * side))
    weights = jnp.where(freqs == 0.0, jnp.sqrt(1.0 / side), jnp.sqrt(2.0 / side))
    return table * weights


def into_blocks(field, side):
    leading = field.shape[:-2]
    depth = len(leading)
    shaped = field.reshape(leading + (field.shape[-2] // side, side, field.shape[-1] // side, side))
    return jnp.moveaxis(shaped, depth + 2, depth + 1)


def out_blocks(blocks):
    leading = blocks.shape[:-4]
    depth = len(leading)
    moved = jnp.moveaxis(blocks, depth + 1, depth + 2)
    return moved.reshape(
        leading + (blocks.shape[-4] * blocks.shape[-2], blocks.shape[-3] * blocks.shape[-1])
    )


def forward_blocks(blocks, table):
    return jnp.einsum("kn,...nm,lm->...kl", table, blocks, table, precision=lax.Precision.HIGHEST)


def inverse_blocks(blocks, table):
    return jnp.einsum("kn,...kl,lm->...nm", table, blocks, table, precision=lax.Precision.HIGHEST)


def scatter_picked(picked, positions, target_shape):
    places = [
        lax.broadcasted_iota(jnp.int32, positions.shape, dimension)
        for dimension in range(positions.ndim - 1)
    ]
    return jnp.zeros(target_shape, picked.dtype).at[tuple(places) + (positions,)].add(picked)


def local(gradients, momentum, master, indices):
    table = cosine_table(BLOCK)
    height = master.shape[0] // BLOCK
    across = master.shape[1] // BLOCK
    local_ids = indices[0]
    local_grad = gradients[0, 0]
    summed = summed_rows(local_grad.astype(jnp.float32), ("shard_0", "shard_1"), "shard_2", 1)
    accumulated = momentum_decay * momentum[0] + summed
    coeffs = forward_blocks(into_blocks(accumulated, BLOCK), table)
    flat = coeffs.reshape(height, across, BLOCK * BLOCK)
    picked = jnp.take_along_axis(flat, local_ids, axis=2)
    own_dense = scatter_picked(picked, local_ids, flat.shape)
    momentum_out = accumulated - out_blocks(inverse_blocks(own_dense.reshape(coeffs.shape), table))
    piece_values = gathered_copies(picked[None], "group", 0)
    piece_ids = gathered_copies(local_ids[None], "group", 0)
    piece_ids = piece_ids.astype(jnp.int32)
    first = lax.broadcasted_iota(jnp.int32, piece_ids.shape, 1)
    second = lax.broadcasted_iota(jnp.int32, piece_ids.shape, 2)
    union_sum = jnp.zeros(flat.shape, jnp.float32).at[first, second, piece_ids].add(piece_values)
    change_field = out_blocks(inverse_blocks(union_sum.reshape(coeffs.shape), table))
    master_out = master - step_rate * jnp.tanh(change_field)
    params_full = lax.all_gather(master_out.astype(jnp.bfloat16), SHARD, axis=1, tiled=True)
    return (momentum_out[None], master_out, params_full)


def solution(mesh):
    torus = Mesh(
        mesh.devices.reshape(mesh.shape["group"], 4, 4, 2),
        ("group", "shard_0", "shard_1", "shard_2"),
    )
    placed = (
        P("group", SHARD, None, None),
        P("group", None, SHARD),
        P(None, SHARD),
        P("group", None, SHARD, None),
    )
    return jax.shard_map(
        local,
        mesh=torus,
        in_specs=placed,
        out_specs=(P("group", None, SHARD), P(None, SHARD), P()),
        check_vma=False,
    )
```

profile of v0, /device:TPU:1, one launch (start us, length us, event | category | flops | bytes accessed | tf_op | source)
XLA Modules:
  0.0 294.3 jit_solution(5407330677718282875)
XLA Ops:
  7.2 6.4 %copy.42 = bf16[1,1,256,8192]{2,3,1,0:T(8,128)(2,1)} copy(bf16[1,1,256,8192]{3,2,1,0:T(8,128)(2,1)} %param.4) | data formatting | bytes 8388608 | tf_op args[0]
  13.6 6.5 %convert.5 = f32[256,32,256]{0,2,1:T(8,128)} convert(bf16[256,32,256]{0,2,1:T(8,128)(2,1)} %bitcast.55) | non-fusion elementwise | flops 2097152 | bytes 12582912 | tf_op jit(solution)/shard_map/reshape | solution.py:22
  20.0 8.7 %copy.44 = f32[2,16,256,256]{3,2,1,0:T(8,128)} copy(f32[2,16,256,256]{2,3,0,1:T(8,128)} %bitcast.54) | data formatting | bytes 16777216 | tf_op jit(solution)/shard_map/reshape | solution.py:22
  28.8 26.3 %reduce-scatter.3.cloned.1.call-done = f32[16,256,256]{2,1,0:T(8,128)} async-done(((f32[32,256,256]{2,1,0:T(8,128)}), f32[16,256,256]{2,1,0:T(8,128)}) %reduce-scatter.3.cloned.1.call-update) | async-done | bytes 4194320 | tf_op jit(solution)/shard_map/reduce_scatter | solution.py:23
  55.1 0.7 reshape.197
  55.9 8.9 %all-to-all-start = ((s32[8,1,512]{2,1,0:T(1,128)}), s32[8,1,512]{2,1,0:T(1,128)S(1)}, u32[]{:S(2)}, u32[]{:S(2)}) async-start(s32[8,1,512]{2,1,0:T(1,128)} %reshape.197), calls=%async_computation.2 | async-start | bytes 32768 | tf_op jit(solution)/shard_map/all_to_all | solution.py:35
  64.9 8.9 %all-to-all-done = s32[8,1,512]{2,1,0:T(1,128)S(1)} async-done(((s32[8,1,512]{2,1,0:T(1,128)}), s32[8,1,512]{2,1,0:T(1,128)S(1)}, u32[]{:S(2)}, u32[]{:S(2)}) %all-to-all-start) | async-done | bytes 16416 | tf_op jit(solution)/shard_map/all_to_all | solution.py:35
  73.8 0.5 broadcast.241
  74.3 0.7 reduce.4
  75.4 81.4 %reduce-scatter.5.cloned.1.call-done = f32[1,256,256]{2,1,0:T(8,128)} async-done(((f32[16,256,256]{2,1,0:T(8,128)}), f32[1,256,256]{2,1,0:T(8,128)}) %reduce-scatter.5.cloned.1.call-update) | async-done | bytes 262160 | tf_op jit(solution)/shard_map/reduce_scatter | solution.py:24
  156.8 1.0 multiply_add_fusion
  158.3 1.7 fusion.2
  160.0 0.7 fusion.12
  160.9 5.3 %gather_fusion = f32[512]{0:T(512)S(1)} fusion(f32[4,4,4096]{2,1,0:T(4,128)S(1)} %reshape.156, s32[512]{0:T(512)S(1)} %reshape.173), kind=kCustom, calls=%fused_computation | custom fusion | bytes 10240 | tf_op jit(solution)/shard_map/jit(take_along_axis)/gather | solution.py:94
  166.3 0.7 reshape.199
  167.0 6.8 %all-to-all-start.1 = ((f32[8,1,512]{2,1,0:T(1,128)}), f32[8,1,512]{2,1,0:T(1,128)S(1)}, u32[]{:S(2)}, u32[]{:S(2)}) async-start(f32[8,1,512]{2,1,0:T(1,128)} %reshape.199), calls=%async_computation.3 | async-start | bytes 32768 | tf_op jit(solution)/shard_map/all_to_all | solution.py:35
  174.0 8.8 %all-to-all-done.1 = f32[8,1,512]{2,1,0:T(1,128)S(1)} async-done(((f32[8,1,512]{2,1,0:T(1,128)}), f32[8,1,512]{2,1,0:T(1,128)S(1)}, u32[]{:S(2)}, u32[]{:S(2)}) %all-to-all-start.1) | async-done | bytes 16416 | tf_op jit(solution)/shard_map/all_to_all | solution.py:35
  182.8 0.5 broadcast.242
  183.3 0.7 reduce.5
  184.2 22.2 %scatter_custom_fusion.1 = f32[65536]{0:T(1024)S(1)} fusion(s32[4096]{0:T(1024)S(1)} %reshape.185, f32[4096]{0:T(1024)S(1)} %reshape.187, f32[]{:T(128)} %constant.16.clone.1), kind=kCustom, calls=%fused_computation.14 | custom fusion | flops 4096 | bytes 262148
  206.5 0.7 fusion.7
  207.3 0.7 fusion.1
  208.0 0.3 copy.54
  208.3 0.3 mul.148
  208.7 0.8 fusion.46
  209.7 30.1 %scatter_fusion = f32[4,4,4096]{2,1,0:T(4,128)S(1)} fusion(f32[4,4,4096]{2,1,0:T(4,128)S(1)} %broadcast.160, s32[512]{0:T(512)S(1)} %reshape.179, f32[512]{0:T(512)S(1)} %reshape.181), kind=kCustom, calls=%fused_computation.1 | custom fusion | flops 512 | bytes 12288 | tf_op jit(solution)/shard_map/scatter-add | solution.py:81
  240.0 0.7 fusion.10
  240.8 0.7 convolution_bitcast_fusion
  241.8 0.3 reshape.158
  242.2 0.7 sub.7
  242.9 40.2 %all-gather.2.cloned.1.call-done = bf16[256,8192]{1,0:T(8,128)(2,1)} async-done(((bf16[256,256]{1,0:T(8,128)(2,1)}), bf16[256,8192]{1,0:T(8,128)(2,1)}) %all-gather.2.cloned.1.call-update) | async-done | bytes 4194320 | tf_op jit(solution)/shard_map/all_gather | solution.py:105
  283.2 4.6 %copy.65 = bf16[256,8192]{1,0:T(8,128)(2,1)} copy(bf16[256,8192]{1,0:T(8,128)(2,1)} %all-gather.2.cloned.1.call-done) | data formatting | bytes 8388608
  (43 shorter events, 2.7 us)
Async XLA Ops:
  7.2 47.9 %reduce-scatter.3.cloned.1.call-start = ((), (), s32[]{:S(2)}) async-start(), calls=%async_computation.4 | async-start | bytes 12582912 | tf_op jit(solution)/shard_map/reduce_scatter | solution.py:23
  28.7 26.4 %copy-start.2 = (s32[1,4,4,32]{3,2,1,0:T(4,128)S(1)}, s32[1,4,4,32]{3,2,1,0:T(4,128)}, u32[]{:S(2)}) copy-start(s32[1,4,4,32]{3,2,1,0:T(4,128)} %param.7) | copy-start | bytes 6148
  28.7 46.4 %copy-start.4 = (s32[3]{0:T(128)S(1)}, s32[3]{0:T(128)}, u32[]{:S(2)}) copy-start(s32[3]{0:T(128)} %constant.53) | copy-start | bytes 40
  28.8 46.5 %copy-start.3 = (s32[3]{0:T(128)S(1)}, s32[3]{0:T(128)}, u32[]{:S(2)}) copy-start(s32[3]{0:T(128)} %constant.56) | copy-start | bytes 40
  28.8 128.0 %copy-start = (f32[1,256,256]{2,1,0:T(8,128)S(1)}, f32[1,256,256]{2,1,0:T(8,128)}, u32[]{:S(2)}) copy-start(f32[1,256,256]{2,1,0:T(8,128)} %param.5) | copy-start | bytes 786436
  28.8 128.0 %reduce-scatter.5.cloned.1.call-start = ((), (), s32[]{:S(2)}) async-start(), calls=%async_computation.5 | async-start | bytes 4456448 | tf_op jit(solution)/shard_map/reduce_scatter | solution.py:24
  55.9 17.9 %all-to-all-start = ((s32[8,1,512]{2,1,0:T(1,128)}), s32[8,1,512]{2,1,0:T(1,128)S(1)}, u32[]{:S(2)}, u32[]{:S(2)}) async-start(s32[8,1,512]{2,1,0:T(1,128)} %reshape.197), calls=%async_computation.2 | async-start | bytes 32768 | tf_op jit(solution)/shard_map/all_to_all | solution.py:35
  166.2 42.5 %copy-start.1 = (f32[256,256]{1,0:T(8,128)S(1)}, f32[256,256]{1,0:T(8,128)}, u32[]{:S(2)}) copy-start(f32[256,256]{1,0:T(8,128)} %param.6) | copy-start | bytes 786436
  167.0 15.8 %all-to-all-start.1 = ((f32[8,1,512]{2,1,0:T(1,128)}), f32[8,1,512]{2,1,0:T(1,128)S(1)}, u32[]{:S(2)}, u32[]{:S(2)}) async-start(f32[8,1,512]{2,1,0:T(1,128)} %reshape.199), calls=%async_computation.3 | async-start | bytes 32768 | tf_op jit(solution)/shard_map/all_to_all | solution.py:35
  173.8 109.3 %all-gather.2.cloned.1.call-start = ((), (), s32[]{:S(2)}) async-start(), calls=%async_computation.6 | async-start | bytes 4325376 | tf_op jit(solution)/shard_map/all_gather | solution.py:105
Sparse Core Ops, SparseCore 0:
  28.9 26.1 reduce-scatter.2
  57.6 99.1 reduce-scatter.4
  209.6 73.5 all-gather.1
where the time goes:
time: 295 us; the launch traced here: 294 us
  waiting for transfers between devices  166 us (56%)
  other arithmetic  62.8 us (21%)
  local copies, waits for them, and re-layouts  30.7 us (10%)
  starting transfers between devices  15.8 us (5%)
  between operations  14 us (5%)
  matrix products  5.28 us (2%)
    reduce_scatter x1, waiting for transfers between devices, summed_rows(): return lax.psum_scatter(parts, chips, scatter_dimension=0, tiled=True)[0]  81.4 us
    all_gather x1, waiting for transfers between devices, local(): lax.all_gather(master_out.astype(jnp.bfloat16), SHARD, axis=1, tiled=True)  40.2 us
    scatter-add x1, other arithmetic, scatter_picked(): jnp.zeros(target_shape, picked.dtype).at[tuple(places) + (positions,)]  30.1 us
    reduce_scatter x1, waiting for transfers between devices, summed_rows(): parts = lax.psum_scatter(parts, core, scatter_dimension=0, tiled=True)  26.3 us
    unnamed x4, other arithmetic  22.4 us
    all_to_all x2, waiting for transfers between devices, copy_for_each(): lax.all_to_all(jnp.broadcast_to(shard[None], (peers, *shard.shape)), axis...  17.7 us
    all_to_all x2, starting transfers between devices, copy_for_each(): lax.all_to_all(jnp.broadcast_to(shard[None], (peers, *shard.shape)), axis...  15.7 us
    unnamed x18, local copies, waits for them, and re-layouts  12.8 us
  transfers between devices with their start and end apart: 5, of which 5 were waited for; matrix products, arithmetic and copies ran while one was open for 12% of the time, Pallas kernels for 0%

commit v1 on v0

--- a/solution.py
+++ b/solution.py
@@ -102,7 +102,11 @@
     union_sum = jnp.zeros(flat.shape, jnp.float32).at[first, second, piece_ids].add(piece_values)
     change_field = out_blocks(inverse_blocks(union_sum.reshape(coeffs.shape), table))
     master_out = master - step_rate * jnp.tanh(change_field)
-    params_full = lax.all_gather(master_out.astype(jnp.bfloat16), SHARD, axis=1, tiled=True)
+    block = master_out.astype(jnp.bfloat16)
+    size = lax.axis_size(SHARD)
+    pieces = jnp.stack([block for _ in range(size)])
+    pieces = lax.all_to_all(pieces, SHARD, split_axis=0, concat_axis=0)
+    params_full = jnp.concatenate(pieces, axis=1)
     return (momentum_out[None], master_out, params_full)
 
 

time: 295 us -> 340 us (1.15)
  waiting for transfers between devices: 166 us -> 186 us
  starting transfers between devices: 15.8 us -> 28.7 us
  local copies, waits for them, and re-layouts: 30.7 us -> 41.3 us
    all_to_all x0 -> x1, waiting for transfers between devices: none -> 61.1 us  [local(): pieces = lax.all_to_all(pieces, SHARD, split_axis=0, concat_axis=0)]
    all_gather x1 -> x0, waiting for transfers between devices: 40.2 us -> none  [local(): lax.all_gather(master_out.astype(jnp.bfloat16), SHARD, axis=1, tiled=True)]
    all_to_all x0 -> x1, starting transfers between devices: none -> 12.9 us  [local(): pieces = lax.all_to_all(pieces, SHARD, split_axis=0, concat_axis=0)]
    all_to_all x0 -> x1, local copies, waits for them, and re-layouts: none -> 6.41 us  [local(): pieces = lax.all_to_all(pieces, SHARD, split_axis=0, concat_axis=0)]
  transfers between devices with their start and end apart: 5 -> 5, of which waited for: 5 -> 5; matrix products, arithmetic and copies ran while one was open for 12% -> 11% of each run, Pallas kernels for 0% -> 0%
where the time goes in v1:
time: 340 us; the launch traced here: 339 us
  waiting for transfers between devices  186 us (55%)
  other arithmetic  62.6 us (18%)
  local copies, waits for them, and re-layouts  41.3 us (12%)
  starting transfers between devices  28.7 us (8%)
  between operations  14.3 us (4%)
  matrix products  5.28 us (2%)
    reduce_scatter x1, waiting for transfers between devices, summed_rows(): return lax.psum_scatter(parts, chips, scatter_dimension=0, tiled=True)[0]  81.4 us
    all_to_all x1, waiting for transfers between devices, local(): pieces = lax.all_to_all(pieces, SHARD, split_axis=0, concat_axis=0)  61.1 us
    scatter-add x1, other arithmetic, scatter_picked(): jnp.zeros(target_shape, picked.dtype).at[tuple(places) + (positions,)]  30.1 us
    reduce_scatter x1, waiting for transfers between devices, summed_rows(): parts = lax.psum_scatter(parts, core, scatter_dimension=0, tiled=True)  26.3 us
    unnamed x4, other arithmetic  22.2 us
    all_to_all x2, waiting for transfers between devices, copy_for_each(): lax.all_to_all(jnp.broadcast_to(shard[None], (peers, *shard.shape)), axis...  17.7 us
    all_to_all x2, starting transfers between devices, copy_for_each(): lax.all_to_all(jnp.broadcast_to(shard[None], (peers, *shard.shape)), axis...  15.7 us
    unnamed x18, local copies, waits for them, and re-layouts  14.4 us
  transfers between devices with their start and end apart: 5, of which 5 were waited for; matrix products, arithmetic and copies ran while one was open for 11% of the time, Pallas kernels for 0%

profile of v1, /device:TPU:1, one launch (start us, length us, event | category | flops | bytes accessed | tf_op | source)
XLA Modules:
  0.0 338.7 jit_solution(10619469186513324801)
XLA Ops:
  7.2 6.4 %copy.42 = bf16[1,1,256,8192]{2,3,1,0:T(8,128)(2,1)} copy(bf16[1,1,256,8192]{3,2,1,0:T(8,128)(2,1)} %param.4) | data formatting | bytes 8388608 | tf_op args[0]
  13.6 6.5 %convert.5 = f32[256,32,256]{0,2,1:T(8,128)} convert(bf16[256,32,256]{0,2,1:T(8,128)(2,1)} %bitcast.58) | non-fusion elementwise | flops 2097152 | bytes 12582912 | tf_op jit(solution)/shard_map/reshape | solution.py:22
  20.0 8.7 %copy.44 = f32[2,16,256,256]{3,2,1,0:T(8,128)} copy(f32[2,16,256,256]{2,3,0,1:T(8,128)} %bitcast.57) | data formatting | bytes 16777216 | tf_op jit(solution)/shard_map/reshape | solution.py:22
  28.8 26.3 %reduce-scatter.3.cloned.1.call-done = f32[16,256,256]{2,1,0:T(8,128)} async-done(((f32[32,256,256]{2,1,0:T(8,128)}), f32[16,256,256]{2,1,0:T(8,128)}) %reduce-scatter.3.cloned.1.call-update) | async-done | bytes 4194320 | tf_op jit(solution)/shard_map/reduce_scatter | solution.py:23
  55.1 0.7 reshape.207
  55.9 8.9 %all-to-all-start = ((s32[8,1,512]{2,1,0:T(1,128)}), s32[8,1,512]{2,1,0:T(1,128)S(1)}, u32[]{:S(2)}, u32[]{:S(2)}) async-start(s32[8,1,512]{2,1,0:T(1,128)} %reshape.207), calls=%async_computation.2 | async-start | bytes 32768 | tf_op jit(solution)/shard_map/all_to_all | solution.py:35
  64.9 8.9 %all-to-all-done = s32[8,1,512]{2,1,0:T(1,128)S(1)} async-done(((s32[8,1,512]{2,1,0:T(1,128)}), s32[8,1,512]{2,1,0:T(1,128)S(1)}, u32[]{:S(2)}, u32[]{:S(2)}) %all-to-all-start) | async-done | bytes 16416 | tf_op jit(solution)/shard_map/all_to_all | solution.py:35
  73.8 0.5 broadcast.243
  74.3 0.7 reduce.4
  75.4 81.4 %reduce-scatter.5.cloned.1.call-done = f32[1,256,256]{2,1,0:T(8,128)} async-done(((f32[16,256,256]{2,1,0:T(8,128)}), f32[1,256,256]{2,1,0:T(8,128)}) %reduce-scatter.5.cloned.1.call-update) | async-done | bytes 262160 | tf_op jit(solution)/shard_map/reduce_scatter | solution.py:24
  156.8 1.0 multiply_add_fusion
  158.3 1.7 fusion.2
  160.0 0.7 fusion.12
  160.9 5.3 %gather_fusion = f32[512]{0:T(512)S(1)} fusion(f32[4,4,4096]{2,1,0:T(4,128)S(1)} %reshape.164, s32[512]{0:T(512)S(1)} %reshape.183), kind=kCustom, calls=%fused_computation | custom fusion | bytes 10240 | tf_op jit(solution)/shard_map/jit(take_along_axis)/gather | solution.py:94
  166.3 0.7 reshape.209
  167.0 6.8 %all-to-all-start.1 = ((f32[8,1,512]{2,1,0:T(1,128)}), f32[8,1,512]{2,1,0:T(1,128)S(1)}, u32[]{:S(2)}, u32[]{:S(2)}) async-start(f32[8,1,512]{2,1,0:T(1,128)} %reshape.209), calls=%async_computation.3 | async-start | bytes 32768 | tf_op jit(solution)/shard_map/all_to_all | solution.py:35
  174.0 8.8 %all-to-all-done.1 = f32[8,1,512]{2,1,0:T(1,128)S(1)} async-done(((f32[8,1,512]{2,1,0:T(1,128)}), f32[8,1,512]{2,1,0:T(1,128)S(1)}, u32[]{:S(2)}, u32[]{:S(2)}) %all-to-all-start.1) | async-done | bytes 16416 | tf_op jit(solution)/shard_map/all_to_all | solution.py:35
  182.8 0.5 broadcast.244
  183.3 0.7 reduce.5
  184.2 22.0 %scatter_custom_fusion.1 = f32[65536]{0:T(1024)S(1)} fusion(s32[4096]{0:T(1024)S(1)} %reshape.195, f32[4096]{0:T(1024)S(1)} %reshape.197, f32[]{:T(128)} %constant.16.clone.1), kind=kCustom, calls=%fused_computation.14 | custom fusion | flops 4096 | bytes 262148
  206.3 0.7 fusion.7
  207.1 0.7 fusion.1
  208.5 0.7 fusion.46
  209.2 2.5 stack.2
  211.7 12.9 %all-to-all-start.2 = ((bf16[32,256,256]{2,1,0:T(8,128)(2,1)}), bf16[32,256,256]{2,1,0:T(8,128)(2,1)}, u32[]{:S(2)}, u32[]{:S(2)}) async-start(bf16[32,256,256]{2,1,0:T(8,128)(2,1)} %stack.2), calls=%async_computation.4 | async-start | bytes 8388608 | tf_op jit(solution)/shard_map/all_to_all | solution.py:108
  224.8 30.1 %scatter_fusion = f32[4,4,4096]{2,1,0:T(4,128)S(1)} fusion(f32[4,4,4096]{2,1,0:T(4,128)S(1)} %broadcast.162, s32[512]{0:T(512)S(1)} %reshape.189, f32[512]{0:T(512)S(1)} %reshape.191), kind=kCustom, calls=%fused_computation.1 | custom fusion | flops 512 | bytes 12288 | tf_op jit(solution)/shard_map/scatter-add | solution.py:81
  255.2 0.8 fusion.10
  256.0 0.7 convolution_bitcast_fusion
  257.4 0.7 sub.7
  258.1 61.1 %all-to-all-done.2 = bf16[32,256,256]{2,1,0:T(8,128)(2,1)} async-done(((bf16[32,256,256]{2,1,0:T(8,128)(2,1)}), bf16[32,256,256]{2,1,0:T(8,128)(2,1)}, u32[]{:S(2)}, u32[]{:S(2)}) %all-to-all-start.2) | async-done | bytes 4194336 | tf_op jit(solution)/shard_map/all_to_all | solution.py:108
  319.1 6.4 %copy.55 = bf16[32,256,256]{1,2,0:T(8,128)(2,1)} copy(bf16[32,256,256]{2,1,0:T(8,128)(2,1)} %all-to-all-done.2) | data formatting | bytes 8388608 | tf_op jit(solution)/shard_map/all_to_all | solution.py:108
  325.6 6.3 %copy.56 = bf16[256,8192]{1,0:T(8,128)(2,1)} copy(bf16[256,8192]{0,1:T(8,128)(2,1)} %bitcast.59) | data formatting | bytes 8388608
  (44 shorter events, 3.7 us)
Async XLA Ops:
  7.2 47.9 %reduce-scatter.3.cloned.1.call-start = ((), (), s32[]{:S(2)}) async-start(), calls=%async_computation.5 | async-start | bytes 12582912 | tf_op jit(solution)/shard_map/reduce_scatter | solution.py:23
  28.7 26.4 %copy-start.2 = (s32[1,4,4,32]{3,2,1,0:T(4,128)S(1)}, s32[1,4,4,32]{3,2,1,0:T(4,128)}, u32[]{:S(2)}) copy-start(s32[1,4,4,32]{3,2,1,0:T(4,128)} %param.7) | copy-start | bytes 6148
  28.7 46.4 %copy-start.4 = (s32[3]{0:T(128)S(1)}, s32[3]{0:T(128)}, u32[]{:S(2)}) copy-start(s32[3]{0:T(128)} %constant.53) | copy-start | bytes 40
  28.8 46.5 %copy-start.3 = (s32[3]{0:T(128)S(1)}, s32[3]{0:T(128)}, u32[]{:S(2)}) copy-start(s32[3]{0:T(128)} %constant.56) | copy-start | bytes 40
  28.8 128.0 %copy-start = (f32[1,256,256]{2,1,0:T(8,128)S(1)}, f32[1,256,256]{2,1,0:T(8,128)}, u32[]{:S(2)}) copy-start(f32[1,256,256]{2,1,0:T(8,128)} %param.5) | copy-start | bytes 786436
  28.8 128.0 %reduce-scatter.5.cloned.1.call-start = ((), (), s32[]{:S(2)}) async-start(), calls=%async_computation.6 | async-start | bytes 4456448 | tf_op jit(solution)/shard_map/reduce_scatter | solution.py:24
  55.9 17.9 %all-to-all-start = ((s32[8,1,512]{2,1,0:T(1,128)}), s32[8,1,512]{2,1,0:T(1,128)S(1)}, u32[]{:S(2)}, u32[]{:S(2)}) async-start(s32[8,1,512]{2,1,0:T(1,128)} %reshape.207), calls=%async_computation.2 | async-start | bytes 32768 | tf_op jit(solution)/shard_map/all_to_all | solution.py:35
  166.2 42.3 %copy-start.1 = (f32[256,256]{1,0:T(8,128)S(1)}, f32[256,256]{1,0:T(8,128)}, u32[]{:S(2)}) copy-start(f32[256,256]{1,0:T(8,128)} %param.6) | copy-start | bytes 786436
  167.0 15.8 %all-to-all-start.1 = ((f32[8,1,512]{2,1,0:T(1,128)}), f32[8,1,512]{2,1,0:T(1,128)S(1)}, u32[]{:S(2)}, u32[]{:S(2)}) async-start(f32[8,1,512]{2,1,0:T(1,128)} %reshape.209), calls=%async_computation.3 | async-start | bytes 32768 | tf_op jit(solution)/shard_map/all_to_all | solution.py:35
  211.7 107.4 %all-to-all-start.2 = ((bf16[32,256,256]{2,1,0:T(8,128)(2,1)}), bf16[32,256,256]{2,1,0:T(8,128)(2,1)}, u32[]{:S(2)}, u32[]{:S(2)}) async-start(bf16[32,256,256]{2,1,0:T(8,128)(2,1)} %stack.2), calls=%async_computation.4 | async-start | bytes 8388608 | tf_op jit(solution)/shard_map/all_to_all | solution.py:108
Sparse Core Ops, SparseCore 0:
  28.9 26.1 reduce-scatter.2
  57.6 99.1 reduce-scatter.4
